TPU v7x, 256 devices: a whole 4x4x8 slice. The times are simulated.
256 devices in a mesh: dp: 8 (over x, core), fsdp: 8 (over z), mp: 4 (over y).
Axes of the slice: x: 4, y: 4, z: 8, core: 2. Of those that a mesh axis runs over, the one named last changes fastest.
Arguments:
- gradients: bfloat16 [64, 12, 2, 256, 1024], P(('dp', 'fsdp'), None, None, None, 'mp'), may hold values from -16 to 16
- master: float32 [12, 2, 256, 1024], P(None, None, ('dp', 'fsdp'), 'mp'), may hold values from -0.375 to 0.375
- teacher: float32 [12, 2, 256, 1024], P(None, None, ('dp', 'fsdp'), 'mp'), may hold values from -0.375 to 0.375
- first_moment: float32 [12, 2, 256, 1024], P(None, None, ('dp', 'fsdp'), 'mp'), may hold values from -2.2888184e-05 to 2.2888184e-05
- second_moment: float32 [12, 2, 256, 1024], P(None, None, ('dp', 'fsdp'), 'mp'), may hold values from 0 to 1, as said below
- layer_rates: float32 [12], replicated, may hold values from 0.02 to 0.2
Outputs:
- master_new: float32 [12, 2, 256, 1024], P(None, None, ('dp', 'fsdp'), 'mp')
- teacher_new: float32 [12, 2, 256, 1024], P(None, None, ('dp', 'fsdp'), 'mp')
- first_new: float32 [12, 2, 256, 1024], P(None, None, ('dp', 'fsdp'), 'mp')
- second_new: float32 [12, 2, 256, 1024], P(None, None, ('dp', 'fsdp'), 'mp')
- student_weights: bfloat16 [12, 2, 256, 1024], P(None, None, None, 'mp')
- teacher_weights: bfloat16 [12, 2, 256, 1024], P(None, None, None, 'mp')
Inputs may be any that keep to these rules, and one draw needn't show every extreme that they name: `second_moment`: every entry is positive.
All inputs are finite; a program needn't handle non-finite values.
Results may differ from a plain program's by a relative error of at most 0.0004.
Values may be sent and summed in bfloat16 or wider, within the bound.
No kernel may reach another device: no remote copies, remote signals or barrier semaphores. Data moves between devices by JAX's collectives and lax.ppermute only.
A program may use at most 64 MiB of HBM per device.

v0:
```python
import jax
import jax.numpy as jnp
from jax import lax
from jax.sharding import PartitionSpec as P

OWN = ("dp", "fsdp")
ALL = ("dp", "fsdp", "mp")
CLIP_NORM = 0.1
BETA_ONE = 0.9
BETA_TWO = 0.999
BIAS_ONE = 1.0 - 0.9**50 * 0.9**50
BIAS_TWO = 1.0 - 0.999**50 * 0.999**50
ADAM_EPS = 1e-08
DECAY = 0.05
EMA_KEEP = 0.95


def shards(gradients, master, teacher, first_moment, second_moment, layer_rates):
    own_grad = gradients[0].astype(jnp.float32)
    summed = lax.psum_scatter(own_grad, OWN, scatter_dimension=2, tiled=True)
    mean_grad = summed / 64.0
    norm_sq = lax.psum(jnp.sum(mean_grad * mean_grad), ALL)
    clip_factor = jnp.minimum(1.0, CLIP_NORM / (jnp.sqrt(norm_sq) + 1e-06))
    clipped = clip_factor * mean_grad
    first_new = BETA_ONE * first_moment + (1.0 - BETA_ONE) * clipped
    second_new = BETA_TWO * second_moment + (1.0 - BETA_TWO) * clipped * clipped
    direction = first_new / BIAS_ONE / (jnp.sqrt(second_new / BIAS_TWO) + ADAM_EPS) + DECAY * master
    layer_rate = layer_rates[:, None, None, None]
    master_new = master - layer_rate * direction
    teacher_new = EMA_KEEP * teacher + (1.0 - EMA_KEEP) * master_new
    student = lax.all_gather(master_new.astype(jnp.bfloat16), OWN, axis=2, tiled=True)
    teach = lax.all_gather(teacher_new.astype(jnp.bfloat16), OWN, axis=2, tiled=True)
    return (master_new, teacher_new, first_new, second_new, student, teach)


def solution(mesh):
    own = P(None, None, OWN, "mp")
    gathered = P(None, None, None, "mp")
    in_specs = (P(OWN, None, None, None, "mp"), own, own, own, own, P())
    out_specs = (own, own, own, own, gathered, gathered)
    return jax.shard_map(shards, mesh=mesh, in_specs=in_specs, out_specs=out_specs, check_vma=False)
```

profile of v0, /device:TPU:1, one launch (start us, length us, event | category | flops | bytes accessed | tf_op | source)
XLA Modules:
  0.0 413.0 jit_solution(480780248336302537)
XLA Ops:
  7.2 0.0 reduce-scatter.2.cloned.1.call-start
  7.2 7.0 %bitcast_convert_fusion = f32[12,2,256,256]{3,0,1,2:T(8,128)} fusion(bf16[1,12,2,256,256]{4,3,2,1,0:T(8,128)(2,1)} %param.6), kind=kLoop, calls=%fused_computation | loop fusion | flops 1572864 | bytes 9437184 | tf_op jit(solution)/shard_map/convert_element_type | solution.py:19
  14.2 0.0 copy-start
  14.2 0.0 copy-start.1
  14.2 0.0 copy-start.2
  14.2 0.0 copy-start.3
  14.2 0.0 copy-start.4
  14.2 0.0 reduce-scatter.2.cloned.1.call-update
  14.3 0.0 all-gather.3.cloned.1.call-start
  14.3 151.8 %reduce-scatter.2.cloned.1.call-done = f32[12,2,4,256]{3,0,1,2:T(8,128)} async-done(((f32[12,2,256,256]{3,0,1,2:T(8,128)}), f32[12,2,4,256]{3,0,1,2:T(8,128)}) %reduce-scatter.2.cloned.1.call-update) | async-done | bytes 98320 | tf_op jit(solution)/shard_map/reduce_scatter | solution.py:20
  166.1 1.5 multiply_reduce_fusion
  167.6 78.7 %psum.7 = f32[]{:T(128)} all-reduce(f32[]{:T(128)} %multiply_reduce_fusion), channel_id=1, replica_groups=mesh['dp'=8,'fsdp'=8,'mp'=4] {'dp','fsdp','mp'}, use_global_device_ids=true, to_apply=%region_2.0 | all-reduce | flops 1 | bytes 8 | tf_op jit(solution)/shard_map/psum | solution.py:22
  247.1 0.0 copy-done
  247.1 0.0 copy-done.1
  247.1 0.0 copy-done.2
  247.1 0.0 copy-done.3
  247.1 0.0 copy-done.4
  247.1 1.1 fusion.5
  248.3 0.7 copy.18
  248.9 0.0 all-gather.3.cloned.1.call-update
  249.0 0.0 all-gather.5.cloned.1.call-start
  249.0 0.7 copy.19
  249.7 0.0 all-gather.5.cloned.1.call-update
  249.7 0.7 copy.20
  250.4 0.7 copy.21
  251.1 0.7 copy.22
  251.8 0.7 copy.23
  252.5 71.5 %all-gather.3.cloned.1.call-done = bf16[12,2,256,256]{3,1,0,2:T(2,128)(2,1)} async-done(((bf16[12,2,4,256]{3,1,0,2:T(2,128)(2,1)}), bf16[12,2,256,256]{3,1,0,2:T(2,128)(2,1)}) %all-gather.3.cloned.1.call-update) | async-done | bytes 3145744 | tf_op jit(solution)/shard_map/all_gather | solution.py:31
  324.1 4.3 %copy.24 = bf16[12,2,256,256]{3,2,1,0:T(8,128)(2,1)} copy(bf16[12,2,256,256]{3,1,0,2:T(2,128)(2,1)} %all-gather.3.cloned.1.call-done) | data formatting | bytes 6291456
  328.4 73.9 %all-gather.5.cloned.1.call-done = bf16[12,2,256,256]{3,1,0,2:T(2,128)(2,1)} async-done(((bf16[12,2,4,256]{3,1,0,2:T(2,128)(2,1)}), bf16[12,2,256,256]{3,1,0,2:T(2,128)(2,1)}) %all-gather.5.cloned.1.call-update) | async-done | bytes 3145744 | tf_op jit(solution)/shard_map/all_gather | solution.py:32
  402.2 4.3 %copy.25 = bf16[12,2,256,256]{3,2,1,0:T(8,128)(2,1)} copy(bf16[12,2,256,256]{3,1,0,2:T(2,128)(2,1)} %all-gather.5.cloned.1.call-done) | data formatting | bytes 6291456
  (1 shorter events, 0.0 us)
Async XLA Ops:
  7.2 158.9 %reduce-scatter.2.cloned.1.call-start = ((), (), s32[]{:S(2)}) async-start(), calls=%async_computation.1 | async-start | bytes 8519680 | tf_op jit(solution)/shard_map/reduce_scatter | solution.py:20
  14.2 232.9 %copy-start = (f32[12,2,4,256]{3,2,1,0:T(4,128)S(1)}, f32[12,2,4,256]{3,2,1,0:T(4,128)}, u32[]{:S(2)}) copy-start(f32[12,2,4,256]{3,2,1,0:T(4,128)} %param.8) | copy-start | bytes 294916
  14.2 232.9 %copy-start.1 = (f32[12,2,4,256]{3,2,1,0:T(4,128)S(1)}, f32[12,2,4,256]{3,2,1,0:T(4,128)}, u32[]{:S(2)}) copy-start(f32[12,2,4,256]{3,2,1,0:T(4,128)} %param.7) | copy-start | bytes 294916
  14.2 232.9 %copy-start.2 = (f32[12,2,4,256]{3,2,1,0:T(4,128)S(1)}, f32[12,2,4,256]{3,2,1,0:T(4,128)}, u32[]{:S(2)}) copy-start(f32[12,2,4,256]{3,2,1,0:T(4,128)} %param.9) | copy-start | bytes 294916
  14.2 232.9 %copy-start.3 = (f32[12,2,4,256]{3,2,1,0:T(4,128)S(1)}, f32[12,2,4,256]{3,2,1,0:T(4,128)}, u32[]{:S(2)}) copy-start(f32[12,2,4,256]{3,2,1,0:T(4,128)} %param.10) | copy-start | bytes 294916
  14.2 232.9 %copy-start.4 = (f32[12]{0:T(128)S(1)}, f32[12]{0:T(128)}, u32[]{:S(2)}) copy-start(f32[12]{0:T(128)} %param.11) | copy-start | bytes 148
  14.3 309.8 %all-gather.3.cloned.1.call-start = ((), (), s32[]{:S(2)}) async-start(), calls=%async_computation.2 | async-start | bytes 3194880 | tf_op jit(solution)/shard_map/all_gather | solution.py:31
  249.0 153.3 %all-gather.5.cloned.1.call-start = ((), (), s32[]{:S(2)}) async-start(), calls=%async_computation.3 | async-start | bytes 3194880 | tf_op jit(solution)/shard_map/all_gather | solution.py:32
Sparse Core Ops, SparseCore 0:
  14.4 151.6 reduce-scatter.1
  249.1 74.9 all-gather.2
  326.8 75.3 all-gather.4
where the time goes:
time: 413 us
  waiting for transfers between devices  297 us (72%)
  blocking collectives  78.7 us (19%)
  between operations  14.5 us (4%)
  local copies, waits for them, and re-layouts  12.7 us (3%)
  other arithmetic  9.68 us (2%)
    reduce_scatter x1, waiting for transfers between devices, shards(): summed = lax.psum_scatter(own_grad, OWN, scatter_dimension=2, tiled=True)  152 us
    psum x1, blocking collectives, shards(): norm_sq = lax.psum(jnp.sum(mean_grad * mean_grad), ALL)  78.7 us
    all_gather x1, waiting for transfers between devices, shards(): lax.all_gather(teacher_new.astype(jnp.bfloat16), OWN, axis=2, tiled=True)  73.9 us
    all_gather x1, waiting for transfers between devices, shards(): lax.all_gather(master_new.astype(jnp.bfloat16), OWN, axis=2, tiled=True)  71.5 us
    unnamed x16, local copies, waits for them, and re-layouts  11.4 us
  transfers between devices with their start and end apart: 3, of which 3 were waited for; matrix products, arithmetic and copies ran while one was open for 2% of the time, Pallas kernels for 0%

commit v1 on v0

--- a/solution.py
+++ b/solution.py
@@ -29,7 +29,9 @@
     master_new = master - layer_rate * direction
     teacher_new = EMA_KEEP * teacher + (1.0 - EMA_KEEP) * master_new
     student = lax.all_gather(master_new.astype(jnp.bfloat16), OWN, axis=2, tiled=True)
-    teach = lax.all_gather(teacher_new.astype(jnp.bfloat16), OWN, axis=2, tiled=True)
+    shard = teacher_new.astype(jnp.bfloat16)
+    copies = jnp.concatenate([shard] * lax.axis_size(OWN), axis=2)
+    teach = lax.all_to_all(copies, OWN, 2, 2, tiled=True)
     return (master_new, teacher_new, first_new, second_new, student, teach)
 
 

time: 413 us -> 419 us (1.015)
  waiting for transfers between devices: 297 us -> 254 us
  local copies, waits for them, and re-layouts: 12.7 us -> 52.7 us
  starting transfers between devices: 0.12 us -> 7.85 us
    all_to_all x0 -> x1, waiting for transfers between devices: none -> 102 us  [shards(): teach = lax.all_to_all(copies, OWN, 2, 2, tiled=True)]
    all_gather x1 -> x0, waiting for transfers between devices: 73.9 us -> none  [shards(): lax.all_gather(teacher_new.astype(jnp.bfloat16), OWN, axis=2, tiled=True)]
    all_gather x1, waiting for transfers between devices: 71.5 us -> 0.01 us  [shards(): lax.all_gather(master_new.astype(jnp.bfloat16), OWN, axis=2, tiled=True)]
    unnamed x16 -> x78, local copies, waits for them, and re-layouts: 11.4 us -> 51.4 us
    all_to_all x0 -> x1, starting transfers between devices: none -> 7.77 us  [shards(): teach = lax.all_to_all(copies, OWN, 2, 2, tiled=True)]
  transfers between devices with their start and end apart: 3 -> 3, of which waited for: 3 -> 2; matrix products, arithmetic and copies ran while one was open for 2% -> 2% of each run, Pallas kernels for 0% -> 0%
where the time goes in v1:
time: 419 us; the launch traced here: 418 us
  waiting for transfers between devices  254 us (61%)
  blocking collectives  78.7 us (19%)
  local copies, waits for them, and re-layouts  52.7 us (13%)
  between operations  14.9 us (4%)
  other arithmetic  10.3 us (2%)
  starting transfers between devices  7.85 us (2%)
    reduce_scatter x1, waiting for transfers between devices, shards(): summed = lax.psum_scatter(own_grad, OWN, scatter_dimension=2, tiled=True)  152 us
    all_to_all x1, waiting for transfers between devices, shards(): teach = lax.all_to_all(copies, OWN, 2, 2, tiled=True)  102 us
    psum x1, blocking collectives, shards(): norm_sq = lax.psum(jnp.sum(mean_grad * mean_grad), ALL)  78.7 us
    unnamed x78, local copies, waits for them, and re-layouts  51.4 us
  transfers between devices with their start and end apart: 3, of which 2 were waited for; matrix products, arithmetic and copies ran while one was open for 2% of the time, Pallas kernels for 0%

profile of v1, /device:TPU:1, one launch (start us, length us, event | category | flops | bytes accessed | tf_op | source)
XLA Modules:
  0.0 418.2 jit_solution(8010870523226407238)
XLA Ops:
  7.2 7.0 %bitcast_convert_fusion = f32[12,2,256,256]{3,0,1,2:T(8,128)} fusion(bf16[1,12,2,256,256]{4,3,2,1,0:T(8,128)(2,1)} %param.6), kind=kLoop, calls=%fused_computation | loop fusion | flops 1572864 | bytes 9437184 | tf_op jit(solution)/shard_map/convert_element_type | solution.py:19
  14.3 151.8 %reduce-scatter.2.cloned.1.call-done = f32[12,2,4,256]{3,0,1,2:T(8,128)} async-done(((f32[12,2,256,256]{3,0,1,2:T(8,128)}), f32[12,2,4,256]{3,0,1,2:T(8,128)}) %reduce-scatter.2.cloned.1.call-update) | async-done | bytes 98320 | tf_op jit(solution)/shard_map/reduce_scatter | solution.py:20
  166.1 1.5 multiply_reduce_fusion
  167.6 78.7 %psum.7 = f32[]{:T(128)} all-reduce(f32[]{:T(128)} %multiply_reduce_fusion), channel_id=1, replica_groups=mesh['dp'=8,'fsdp'=8,'mp'=4] {'dp','fsdp','mp'}, use_global_device_ids=true, to_apply=%region_2.0 | all-reduce | flops 1 | bytes 8 | tf_op jit(solution)/shard_map/psum | solution.py:22
  247.1 1.7 constant_dynamic-update-slice_fusion.63
  250.1 0.6 constant_dynamic-update-slice_fusion.60
  250.7 0.6 constant_dynamic-update-slice_fusion.59
  251.4 0.6 constant_dynamic-update-slice_fusion.58
  252.0 0.6 constant_dynamic-update-slice_fusion.57
  252.6 0.6 constant_dynamic-update-slice_fusion.56
  253.2 0.6 constant_dynamic-update-slice_fusion.55
  254.5 0.6 constant_dynamic-update-slice_fusion.53
  255.1 0.6 constant_dynamic-update-slice_fusion.52
  256.3 0.6 constant_dynamic-update-slice_fusion.50
  257.6 0.6 constant_dynamic-update-slice_fusion.48
  258.2 0.6 constant_dynamic-update-slice_fusion.47
  259.5 0.6 constant_dynamic-update-slice_fusion.45
  260.1 0.6 constant_dynamic-update-slice_fusion.44
  260.7 0.6 constant_dynamic-update-slice_fusion.43
  261.4 0.6 constant_dynamic-update-slice_fusion.42
  262.0 0.6 constant_dynamic-update-slice_fusion.41
  262.6 0.6 constant_dynamic-update-slice_fusion.40
  263.2 0.6 constant_dynamic-update-slice_fusion.39
  263.9 0.6 constant_dynamic-update-slice_fusion.38
  264.5 0.6 constant_dynamic-update-slice_fusion.37
  265.1 0.6 constant_dynamic-update-slice_fusion.36
  265.7 0.6 constant_dynamic-update-slice_fusion.35
  266.4 0.6 constant_dynamic-update-slice_fusion.34
  267.0 0.6 constant_dynamic-update-slice_fusion.33
  268.2 0.6 constant_dynamic-update-slice_fusion.31
  268.9 0.6 constant_dynamic-update-slice_fusion.30
  269.5 0.6 constant_dynamic-update-slice_fusion.29
  270.1 0.6 constant_dynamic-update-slice_fusion.28
  270.7 0.6 constant_dynamic-update-slice_fusion.27
  271.4 0.6 constant_dynamic-update-slice_fusion.26
  272.0 0.6 constant_dynamic-update-slice_fusion.25
  272.6 0.6 constant_dynamic-update-slice_fusion.24
  273.2 0.6 constant_dynamic-update-slice_fusion.23
  273.9 0.6 constant_dynamic-update-slice_fusion.22
  274.5 0.6 constant_dynamic-update-slice_fusion.21
  275.7 0.6 constant_dynamic-update-slice_fusion.19
  277.0 0.6 constant_dynamic-update-slice_fusion.17
  277.6 0.6 constant_dynamic-update-slice_fusion.16
  278.2 0.6 constant_dynamic-update-slice_fusion.15
  278.9 0.6 constant_dynamic-update-slice_fusion.14
  280.1 0.6 constant_dynamic-update-slice_fusion.12
  280.7 0.6 constant_dynamic-update-slice_fusion.11
  282.6 0.6 constant_dynamic-update-slice_fusion.8
  283.2 0.6 constant_dynamic-update-slice_fusion.7
  283.8 0.6 constant_dynamic-update-slice_fusion.6
  284.5 0.6 constant_dynamic-update-slice_fusion.5
  285.7 0.6 constant_dynamic-update-slice_fusion.3
  286.3 0.6 constant_dynamic-update-slice_fusion.2
  287.0 0.6 constant_dynamic-update-slice_fusion.1
  287.6 0.6 constant_dynamic-update-slice_fusion
  288.2 7.8 %all-to-all-start = ((bf16[12,2,256,256]{3,0,1,2:T(8,128)(2,1)}), bf16[12,2,256,256]{3,0,1,2:T(8,128)(2,1)}, u32[]{:S(2)}, u32[]{:S(2)}) async-start(bf16[12,2,256,256]{3,0,1,2:T(8,128)(2,1)} %constant_dynamic-update-slice_fusion), calls=%async_computation.1 | async-start | bytes 8388608 | tf_op jit(solution)/shard_map/all_to_all | solution.py:34
  296.1 0.7 copy.32
  296.8 0.7 copy.33
  297.5 0.7 copy.34
  298.2 0.7 copy.35
  298.9 0.7 copy.36
  299.6 101.9 %all-to-all-done = bf16[12,2,256,256]{3,0,1,2:T(8,128)(2,1)} async-done(((bf16[12,2,256,256]{3,0,1,2:T(8,128)(2,1)}), bf16[12,2,256,256]{3,0,1,2:T(8,128)(2,1)}, u32[]{:S(2)}, u32[]{:S(2)}) %all-to-all-start) | async-done | bytes 3145760 | tf_op jit(solution)/shard_map/all_to_all | solution.py:34
  401.5 5.6 %copy.38 = bf16[12,2,256,256]{3,2,1,0:T(8,128)(2,1)} copy(bf16[12,2,256,256]{3,0,1,2:T(8,128)(2,1)} %all-to-all-done) | data formatting | bytes 6291456
  407.1 4.3 %copy.37 = bf16[12,2,256,256]{3,2,1,0:T(8,128)(2,1)} copy(bf16[12,2,256,256]{3,1,0,2:T(2,128)(2,1)} %all-gather.2.cloned.1.call-done) | data formatting | bytes 6291456
  (29 shorter events, 8.2 us)
Async XLA Ops:
  7.2 158.9 %reduce-scatter.2.cloned.1.call-start = ((), (), s32[]{:S(2)}) async-start(), calls=%async_computation.2 | async-start | bytes 8519680 | tf_op jit(solution)/shard_map/reduce_scatter | solution.py:20
  14.2 232.9 %copy-start = (f32[12,2,4,256]{3,2,1,0:T(4,128)S(1)}, f32[12,2,4,256]{3,2,1,0:T(4,128)}, u32[]{:S(2)}) copy-start(f32[12,2,4,256]{3,2,1,0:T(4,128)} %param.8) | copy-start | bytes 294916
  14.2 232.9 %copy-start.1 = (f32[12,2,4,256]{3,2,1,0:T(4,128)S(1)}, f32[12,2,4,256]{3,2,1,0:T(4,128)}, u32[]{:S(2)}) copy-start(f32[12,2,4,256]{3,2,1,0:T(4,128)} %param.7) | copy-start | bytes 294916
  14.2 232.9 %copy-start.2 = (f32[12,2,4,256]{3,2,1,0:T(4,128)S(1)}, f32[12,2,4,256]{3,2,1,0:T(4,128)}, u32[]{:S(2)}) copy-start(f32[12,2,4,256]{3,2,1,0:T(4,128)} %param.9) | copy-start | bytes 294916
  14.2 232.9 %copy-start.3 = (f32[12,2,4,256]{3,2,1,0:T(4,128)S(1)}, f32[12,2,4,256]{3,2,1,0:T(4,128)}, u32[]{:S(2)}) copy-start(f32[12,2,4,256]{3,2,1,0:T(4,128)} %param.10) | copy-start | bytes 294916
  14.2 232.9 %copy-start.4 = (f32[12]{0:T(128)S(1)}, f32[12]{0:T(128)}, u32[]{:S(2)}) copy-start(f32[12]{0:T(128)} %param.11) | copy-start | bytes 148
  288.2 113.3 %all-to-all-start = ((bf16[12,2,256,256]{3,0,1,2:T(8,128)(2,1)}), bf16[12,2,256,256]{3,0,1,2:T(8,128)(2,1)}, u32[]{:S(2)}, u32[]{:S(2)}) async-start(bf16[12,2,256,256]{3,0,1,2:T(8,128)(2,1)} %constant_dynamic-update-slice_fusion), calls=%async_computation.1 | async-start | bytes 8388608 | tf_op jit(solution)/shard_map/all_to_all | solution.py:34
  296.0 111.1 %all-gather.2.cloned.1.call-start = ((), (), s32[]{:S(2)}) async-start(), calls=%async_computation.3 | async-start | bytes 3194880 | tf_op jit(solution)/shard_map/all_gather | solution.py:31
Sparse Core Ops, SparseCore 0:
  14.4 151.6 reduce-scatter.1
  300.2 96.6 all-gather.1

commit v2 on v0

--- a/solution.py
+++ b/solution.py
@@ -28,7 +28,12 @@
     layer_rate = layer_rates[:, None, None, None]
     master_new = master - layer_rate * direction
     teacher_new = EMA_KEEP * teacher + (1.0 - EMA_KEEP) * master_new
-    student = lax.all_gather(master_new.astype(jnp.bfloat16), OWN, axis=2, tiled=True)
+    student = jnp.concatenate(
+        lax.all_to_all(
+            jnp.stack([master_new.astype(jnp.bfloat16)] * lax.axis_size(OWN)), OWN, 0, 0
+        ),
+        axis=2,
+    )
     teach = lax.all_gather(teacher_new.astype(jnp.bfloat16), OWN, axis=2, tiled=True)
     return (master_new, teacher_new, first_new, second_new, student, teach)
 

time: 413 us -> 361 us (0.87)
  waiting for transfers between devices: 297 us -> 230 us
  starting transfers between devices: 0.12 us -> 7.65 us
  local copies, waits for them, and re-layouts: 12.7 us -> 18.2 us
    all_to_all x0 -> x1, waiting for transfers between devices: none -> 74.4 us  [shards(): lax.all_to_all(jnp.stack([master_new.astype(jnp.bfloat16)] * lax.axis_siz...]
    all_gather x1 -> x0, waiting for transfers between devices: 71.5 us -> none  [shards(): lax.all_gather(master_new.astype(jnp.bfloat16), OWN, axis=2, tiled=True)]
    all_gather x1, waiting for transfers between devices: 73.9 us -> 4.22 us  [shards(): lax.all_gather(teacher_new.astype(jnp.bfloat16), OWN, axis=2, tiled=True)]
    all_to_all x0 -> x1, starting transfers between devices: none -> 7.58 us  [shards(): lax.all_to_all(jnp.stack([master_new.astype(jnp.bfloat16)] * lax.axis_siz...]
  transfers between devices with their start and end apart: 3 -> 3, of which waited for: 3 -> 3; matrix products, arithmetic and copies ran while one was open for 2% -> 3% of each run, Pallas kernels for 0% -> 0%
where the time goes in v2:
time: 361 us; the launch traced here: 360 us
  waiting for transfers between devices  230 us (64%)
  blocking collectives  78.7 us (22%)
  local copies, waits for them, and re-layouts  18.2 us (5%)
  between operations  14.9 us (4%)
  other arithmetic  10.4 us (3%)
  starting transfers between devices  7.65 us (2%)
    reduce_scatter x1, waiting for transfers between devices, shards(): summed = lax.psum_scatter(own_grad, OWN, scatter_dimension=2, tiled=True)  152 us
    psum x1, blocking collectives, shards(): norm_sq = lax.psum(jnp.sum(mean_grad * mean_grad), ALL)  78.7 us
    all_to_all x1, waiting for transfers between devices, shards(): lax.all_to_all(jnp.stack([master_new.astype(jnp.bfloat16)] * lax.axis_siz...  74.4 us
    unnamed x16, local copies, waits for them, and re-layouts  10.3 us
    all_to_all x1, starting transfers between devices, shards(): lax.all_to_all(jnp.stack([master_new.astype(jnp.bfloat16)] * lax.axis_siz...  7.58 us
  transfers between devices with their start and end apart: 3, of which 3 were waited for; matrix products, arithmetic and copies ran while one was open for 3% of the time, Pallas kernels for 0%

profile of v2, /device:TPU:1, one launch (start us, length us, event | category | flops | bytes accessed | tf_op | source)
XLA Modules:
  0.0 360.3 jit_solution(17079457311985119159)
XLA Ops:
  7.2 0.0 reduce-scatter.2.cloned.1.call-start
  7.2 7.0 %bitcast_convert_fusion = f32[12,2,256,256]{3,0,1,2:T(8,128)} fusion(bf16[1,12,2,256,256]{4,3,2,1,0:T(8,128)(2,1)} %param.6), kind=kLoop, calls=%fused_computation | loop fusion | flops 1572864 | bytes 9437184 | tf_op jit(solution)/shard_map/convert_element_type | solution.py:19
  14.2 0.0 copy-start
  14.2 0.0 copy-start.1
  14.2 0.0 copy-start.2
  14.2 0.0 copy-start.3
  14.2 0.0 copy-start.4
  14.2 0.0 reduce-scatter.2.cloned.1.call-update
  14.3 151.8 %reduce-scatter.2.cloned.1.call-done = f32[12,2,4,256]{3,0,1,2:T(8,128)} async-done(((f32[12,2,256,256]{3,0,1,2:T(8,128)}), f32[12,2,4,256]{3,0,1,2:T(8,128)}) %reduce-scatter.2.cloned.1.call-update) | async-done | bytes 98320 | tf_op jit(solution)/shard_map/reduce_scatter | solution.py:20
  166.1 1.5 multiply_reduce_fusion
  167.6 78.7 %psum.7 = f32[]{:T(128)} all-reduce(f32[]{:T(128)} %multiply_reduce_fusion), channel_id=1, replica_groups=mesh['dp'=8,'fsdp'=8,'mp'=4] {'dp','fsdp','mp'}, use_global_device_ids=true, to_apply=%region_2.0 | all-reduce | flops 1 | bytes 8 | tf_op jit(solution)/shard_map/psum | solution.py:22
  247.1 0.0 copy-done
  247.1 0.0 copy-done.1
  247.1 0.0 copy-done.2
  247.1 0.0 copy-done.3
  247.1 0.0 copy-done.4
  247.1 1.8 fusion.5
  249.0 3.2 stack.2
  252.2 7.6 %all-to-all-start = ((bf16[64,12,2,4,256]{4,3,2,1,0:T(4,128)(2,1)}), bf16[64,12,2,4,256]{4,3,2,1,0:T(4,128)(2,1)S(1)}, u32[]{:S(2)}, u32[]{:S(2)}) async-start(bf16[64,12,2,4,256]{4,3,2,1,0:T(4,128)(2,1)} %stack.2), calls=%async_computation.1 | async-start | bytes 6291456 | tf_op jit(solution)/shard_map/all_to_all | solution.py:32
  259.8 0.0 all-gather.2.cloned.1.call-start
  259.8 1.5 copy.33
  261.3 0.0 all-gather.2.cloned.1.call-update
  261.3 0.7 copy.34
  262.0 1.6 copy.35
  263.6 0.7 copy.36
  264.3 0.7 copy.37
  265.1 74.4 %all-to-all-done = bf16[64,12,2,4,256]{4,3,2,1,0:T(4,128)(2,1)S(1)} async-done(((bf16[64,12,2,4,256]{4,3,2,1,0:T(4,128)(2,1)}), bf16[64,12,2,4,256]{4,3,2,1,0:T(4,128)(2,1)S(1)}, u32[]{:S(2)}, u32[]{:S(2)}) %all-to-all-start) | async-done | bytes 3145760 | tf_op jit(solution)/shard_map/all_to_all | solution.py:32
  339.5 3.2 copy.32
  342.7 2.2 copy.38
  344.9 4.2 %all-gather.2.cloned.1.call-done = bf16[12,2,256,256]{3,1,0,2:T(2,128)(2,1)} async-done(((bf16[12,2,4,256]{3,1,0,2:T(2,128)(2,1)}), bf16[12,2,256,256]{3,1,0,2:T(2,128)(2,1)}) %all-gather.2.cloned.1.call-update) | async-done | bytes 3145744 | tf_op jit(solution)/shard_map/all_gather | solution.py:37
  349.2 4.3 %copy.39 = bf16[12,2,256,256]{3,2,1,0:T(8,128)(2,1)} copy(bf16[12,2,256,256]{3,1,0,2:T(2,128)(2,1)} %all-gather.2.cloned.1.call-done) | data formatting | bytes 6291456
  (2 shorter events, 0.1 us)
Async XLA Ops:
  7.2 158.9 %reduce-scatter.2.cloned.1.call-start = ((), (), s32[]{:S(2)}) async-start(), calls=%async_computation.2 | async-start | bytes 8519680 | tf_op jit(solution)/shard_map/reduce_scatter | solution.py:20
  14.2 232.9 %copy-start = (f32[12,2,4,256]{3,2,1,0:T(4,128)S(1)}, f32[12,2,4,256]{3,2,1,0:T(4,128)}, u32[]{:S(2)}) copy-start(f32[12,2,4,256]{3,2,1,0:T(4,128)} %param.8) | copy-start | bytes 294916
  14.2 232.9 %copy-start.1 = (f32[12,2,4,256]{3,2,1,0:T(4,128)S(1)}, f32[12,2,4,256]{3,2,1,0:T(4,128)}, u32[]{:S(2)}) copy-start(f32[12,2,4,256]{3,2,1,0:T(4,128)} %param.7) | copy-start | bytes 294916
  14.2 232.9 %copy-start.2 = (f32[12,2,4,256]{3,2,1,0:T(4,128)S(1)}, f32[12,2,4,256]{3,2,1,0:T(4,128)}, u32[]{:S(2)}) copy-start(f32[12,2,4,256]{3,2,1,0:T(4,128)} %param.9) | copy-start | bytes 294916
  14.2 232.9 %copy-start.3 = (f32[12,2,4,256]{3,2,1,0:T(4,128)S(1)}, f32[12,2,4,256]{3,2,1,0:T(4,128)}, u32[]{:S(2)}) copy-start(f32[12,2,4,256]{3,2,1,0:T(4,128)} %param.10) | copy-start | bytes 294916
  14.2 232.9 %copy-start.4 = (f32[12]{0:T(128)S(1)}, f32[12]{0:T(128)}, u32[]{:S(2)}) copy-start(f32[12]{0:T(128)} %param.11) | copy-start | bytes 148
  252.2 87.3 %all-to-all-start = ((bf16[64,12,2,4,256]{4,3,2,1,0:T(4,128)(2,1)}), bf16[64,12,2,4,256]{4,3,2,1,0:T(4,128)(2,1)S(1)}, u32[]{:S(2)}, u32[]{:S(2)}) async-start(bf16[64,12,2,4,256]{4,3,2,1,0:T(4,128)(2,1)} %stack.2), calls=%async_computation.1 | async-start | bytes 6291456 | tf_op jit(solution)/shard_map/all_to_all | solution.py:32
  259.8 89.4 %all-gather.2.cloned.1.call-start = ((), (), s32[]{:S(2)}) async-start(), calls=%async_computation.3 | async-start | bytes 3194880 | tf_op jit(solution)/shard_map/all_gather | solution.py:37
Sparse Core Ops, SparseCore 0:
  14.4 151.6 reduce-scatter.1
  263.3 85.7 all-gather.1
